TPU v7x, 32 devices: a whole 2x2x4 slice. The times are simulated.
32 devices in a mesh: group: 2 (over y), tensor: 4 (over z), seq: 4 (over x, core).
Axes of the slice: x: 2, y: 2, z: 4, core: 2. Of those that a mesh axis runs over, the one named last changes fastest.
Arguments:
- mixer_input: bfloat16 [2048, 8192], P(('group', 'seq'), 'tensor'), parts along dimension 0, may hold values from -6 to 6
- state_maps: bfloat16 [2048, 256], P(('group', 'seq')), parts along dimension 0, may hold values from -6 to 6
- gate_input: bfloat16 [2048, 8192], P(('group', 'seq'), 'tensor'), parts along dimension 0, may hold values from -6 to 6
- step_raw: float32 [128, 2048], P('tensor', ('group', 'seq')), parts along dimension 1, may hold values from -10 to 10, as said below
- decay_log: float32 [128], P('tensor'), may hold values from -4 to -2
- skip_gain: float32 [128], P('tensor'), may hold values from 0.5 to 1.5
- conv_input: bfloat16 [4, 8192], P(None, 'tensor'), may hold values from -3 to 3
- conv_maps: bfloat16 [4, 256], replicated, may hold values from -3 to 3
- norm_gain: float32 [8192], P('tensor'), may hold values from 0.1 to 1.9
- out_weight: bfloat16 [8192, 8192], P('tensor'), may hold values from -0.09375 to 0.09375
Outputs:
- mixed: bfloat16 [2048, 8192], P(('group', 'seq'), 'tensor'), parts along dimension 0
There are 2 independent parts, one for each index of `group`. A program takes and returns all parts, laid end to end along the dimension named above; an argument that names none is the same for every part. Nothing has to cross between parts.
Inputs may be any that keep to these rules, and one draw needn't show every extreme that they name: `step_raw`: Real-valued step parameters before softplus.
All inputs are finite; a program needn't handle non-finite values.
Results may differ from a plain program's by a relative error of at most 0.008.
Values may be sent and summed in bfloat16 or wider, within the bound.
A program may use at most 128 MiB of HBM per device.

v0:
```python
import jax
import jax.numpy as jnp
from jax import lax
from jax.sharding import PartitionSpec as P

SPAN = 256


PRECISE = lax.Precision.HIGHEST


def shifted(shard, axis, by):
    devices = lax.axis_size(axis)
    pairs = [(i, i + by) for i in range(devices) if 0 <= i + by < devices]
    return lax.ppermute(shard, axis, pairs)


def entering(value, axis, join, neutral):
    count, mine = (lax.axis_size(axis), lax.axis_index(axis))
    pieces = jax.tree.map(lambda part: lax.all_gather(part, axis), value)
    running = jax.tree.map(
        lambda part, zero: jnp.full_like(part, 0) + jnp.asarray(zero, part.dtype), value, neutral
    )

    def step(position, running):
        longer = join(running, jax.tree.map(lambda part: part[position], pieces))
        return jax.tree.map(lambda new, old: jnp.where(position < mine, new, old), longer, running)

    return lax.fori_loop(0, count - 1, step, running)


def causal_conv(leading, values, kernel):
    padded = jnp.concatenate([leading, values], axis=0).astype(jnp.float32)
    summed = jnp.zeros(values.shape, jnp.float32)
    for offset in range(kernel.shape[0]):
        summed = (
            summed + kernel[offset].astype(jnp.float32) * padded[offset : offset + values.shape[0]]
        )
    return jax.nn.silu(summed).astype(jnp.bfloat16)


def chain_combine(earlier, latter):
    return (earlier[0] * latter[0], latter[0][:, None, None] * earlier[1] + latter[1])


def local(
    mixer_input,
    state_maps,
    gate_input,
    step_raw,
    decay_log,
    skip_gain,
    conv_input,
    conv_maps,
    norm_gain,
    out_weight,
):
    tokens, channels = mixer_input.shape
    resident_heads = decay_log.shape[0]
    head_dim = channels // resident_heads
    state_dim = state_maps.shape[1] // 2
    lead_rows = conv_input.shape[0] - 1
    blocks = tokens // SPAN
    tail_rows = jnp.concatenate(
        [mixer_input[tokens - lead_rows :], state_maps[tokens - lead_rows :]], axis=1
    )
    leading = shifted(tail_rows, "seq", 1)
    conv_out = causal_conv(leading[:, :channels], mixer_input, conv_input)
    maps_out = causal_conv(leading[:, channels:], state_maps, conv_maps)
    b_blocks = maps_out[:, :state_dim].reshape(blocks, SPAN, state_dim)
    c_blocks = maps_out[:, state_dim:].reshape(blocks, SPAN, state_dim)
    scores = jnp.einsum("ktn,ksn->kts", c_blocks, b_blocks, preferred_element_type=jnp.float32)
    step_size = jax.nn.softplus(step_raw)
    step_blocks = step_size.reshape(resident_heads, blocks, SPAN)
    log_decay = -jnp.exp(decay_log)[:, None] * step_size
    cumulative = jnp.cumsum(log_decay.reshape(resident_heads, blocks, SPAN), axis=2)
    causal = lax.broadcasted_iota(jnp.int32, (SPAN, SPAN), 0) >= lax.broadcasted_iota(
        jnp.int32, (SPAN, SPAN), 1
    )
    logarithm_spacing = jnp.where(
        causal, cumulative[:, :, :, None] - cumulative[:, :, None, :], 0.0
    )
    weights = jnp.where(
        causal, scores[None] * jnp.exp(logarithm_spacing) * step_blocks[:, :, None, :], 0.0
    ).astype(jnp.bfloat16)
    value_blocks = conv_out.reshape(blocks, SPAN, resident_heads, head_dim)
    inside = jnp.einsum(
        "hkts,kshp->kthp", weights, value_blocks, preferred_element_type=jnp.float32
    )
    tail_weight = jnp.exp(cumulative[:, :, -1:] - cumulative) * step_blocks
    weighted = value_blocks.astype(jnp.float32) * tail_weight.transpose(1, 2, 0)[:, :, :, None]
    block_states = jnp.einsum(
        "kshp,ksn->khpn", weighted, b_blocks.astype(jnp.float32), precision=PRECISE
    )

    def advance(carried_in, element):
        state_now, prefix = carried_in
        decay_now, block_add = element
        return (
            (decay_now[:, None, None] * state_now + block_add, prefix * decay_now),
            (state_now, prefix),
        )

    zero_state = jnp.zeros((resident_heads, head_dim, state_dim), jnp.float32)
    start_carry = (zero_state, jnp.ones((resident_heads,), jnp.float32))
    (local_end, device_decay), (local_before, prefixes) = lax.scan(
        advance, start_carry, (jnp.exp(cumulative[:, :, -1]).T, block_states)
    )
    identity = (jnp.ones_like(device_decay), zero_state)
    incoming = entering((device_decay, local_end), "seq", chain_combine, identity)[1]
    carried = local_before + prefixes[:, :, None, None] * incoming[None]
    growth = jnp.exp(cumulative).transpose(1, 2, 0)[:, :, :, None]
    carried_part = (
        jnp.einsum("ktn,khpn->kthp", c_blocks.astype(jnp.float32), carried, precision=PRECISE)
        * growth
    )
    scanned = (
        inside + carried_part + skip_gain[None, None, :, None] * value_blocks.astype(jnp.float32)
    )
    gate_values = jax.nn.silu(gate_input.astype(jnp.float32)).reshape(
        tokens, resident_heads, head_dim
    )
    gated_values = scanned.reshape(tokens, resident_heads, head_dim) * gate_values
    inverse_root_mean = lax.rsqrt(
        jnp.mean(gated_values * gated_values, axis=2, keepdims=True) + 1e-05
    )
    normed = ((gated_values * inverse_root_mean).reshape(tokens, channels) * norm_gain).astype(
        jnp.bfloat16
    )
    owned_rows = lax.psum_scatter(
        lax.dot_general(
            out_weight, normed, (((0,), (1,)), ((), ())), preferred_element_type=jnp.float32
        ),
        "tensor",
        scatter_dimension=0,
        tiled=True,
    )
    return owned_rows.T.astype(jnp.bfloat16)


def solution(mesh):
    placed = (
        P(("group", "seq"), "tensor"),
        P(("group", "seq"), None),
        P(("group", "seq"), "tensor"),
        P("tensor", ("group", "seq")),
        P("tensor"),
        P("tensor"),
        P(None, "tensor"),
        P(),
        P("tensor"),
        P("tensor", None),
    )
    return jax.shard_map(
        local, mesh=mesh, in_specs=placed, out_specs=P(("group", "seq"), "tensor"), check_vma=False
    )
```

profile of v0, /device:TPU:11, one launch (start us, length us, event | category | flops | bytes accessed | tf_op | source)
XLA Modules:
  0.0 241.4 jit_solution(11216180270187855887)
XLA Ops:
  6.5 0.0 all-gather.4.cloned.1.call-start
  6.5 0.8 slice.78
  7.3 0.8 slice.77
  8.1 1.3 collective-permute-start
  9.4 0.7 exponential_negate_fusion
  10.1 0.8 compare_select_fusion
  10.9 0.6 reduce-window.6
  11.5 0.2 slice_reduce_fusion
  11.8 0.9 slice_convert_fusion.3
  12.7 0.1 copy.39
  12.8 0.1 broadcast.99
  12.9 0.1 exponential_bitcast_fusion
  13.0 0.6 multiply_reduce_fusion
  13.6 0.8 multiply_bitcast_fusion
  14.4 0.8 slice_convert_fusion.7
  15.2 1.5 copy.36
  16.7 0.0 collective-permute-done
  16.8 0.0 copy-done.2
  16.8 0.3 copy.35
  17.1 0.7 maximum_convert_fusion
  17.8 0.2 multiply_convert_fusion.1
  18.0 3.8 %bitcast_multiply_fusion.3 = (f32[256,2048]{0,1:T(8,128)S(1)}, bf16[256,2048]{0,1:T(8,128)(2,1)}) fusion(f32[256,32]{0,1:T(8,128)S(1)} %get-tuple-element.156, f32[259,2048]{0,1:T(8,128)S(1)} %maximum_convert_fusion, f32[2048]{0:T(1024)S(1)} %bitcast.104, f32[2048]{0:T(1024)S(1)} %bitcast.105, f32[2048]{0:T(1024)S(1)} %bitcast.103, f32[2048]{0:T(1024)S(1)} %bitcast.102), kind=kLoop, calls=%fused_computation.33 | loop fusion | flops 7340032 | bytes 11599872 | tf_op jit(solution)/shard_map/mul | solution.py:91
  21.9 2.0 convolution_add_fusion
  23.9 0.0 all-gather.4.cloned.1.call-update
  23.9 0.0 reduce-scatter.2.cloned.1.call-start
  24.0 0.0 copy-done.5
  24.0 0.7 dynamic-slice.1
  25.4 0.2 dynamic-update-slice
  25.7 6.6 %all-reduce = f32[128]{0:T(128)S(1)} all-reduce(f32[128]{0:T(128)S(1)} %dynamic-update-slice), channel_id=2, replica_groups=mesh['group'=2,'tensor'=4,'seq'=4] {'seq'}, use_global_device_ids=true, to_apply=%add | all-reduce | flops 128 | bytes 1024
  32.2 0.1 reshape.231
  32.3 0.5 copy.41
  32.9 0.2 fusion.26
  33.1 27.1 %all-gather.4.cloned.1.call-done = f32[128,64,128]{2,1,0:T(8,128)} async-done(((f32[32,64,128]{2,1,0:T(8,128)}), f32[128,64,128]{2,1,0:T(8,128)}) %all-gather.4.cloned.1.call-update) | async-done | bytes 4194320 | tf_op jit(solution)/shard_map/all_gather | solution.py:20
  60.1 4.5 %while.9 = (s32[]{:T(128)}, f32[32,64,128]{2,1,0:T(8,128)S(1)}, s32[]{:T(128)}, f32[4,32]{1,0:T(4,128)S(1)}, f32[4,32,64,128]{3,2,1,0:T(8,128)}, /*index=5*/s32[]{:T(128)}, s32[]{:T(128)}) while((s32[]{:T(128)}, f32[32,64,128]{2,1,0:T(8,128)S(1)}, s32[]{:T(128)}, f32[4,32]{1,0:T(4,128)S(1)}, f32[4,32,64,128]{3,2,1,0:T(8,128)}, ...), condition=%wide.region_3.4_spmd.clone, body=%wide.region_2.3_spmd.clone.sunk | while | flops 1048580 | bytes 3146225 | solution.py:29
  60.1 1.5 fusion.38
  61.6 1.5 fusion.38
  63.1 1.5 fusion.38
  64.6 0.0 copy-start.1
  64.6 0.0 copy-start.4
  64.6 1.0 fusion.23
  65.6 0.2 copy-done.1
  65.8 0.0 copy-done.4
  65.8 3.3 %fusion.18 = (f32[256,32]{0,1:T(8,128)S(1)}, f32[1,256,32,64]{1,3,2,0:T(8,128)S(1)}) fusion(bf16[256,2048]{0,1:T(8,128)(2,1)S(1)} %copy.41, f32[32]{0:T(128)S(1)} %copy-done.4, f32[256,32,64]{0,2,1:T(8,128)S(1)} %fusion.23, f32[256,32]{0,1:T(8,128)S(1)} %bitcast.101, bf16[256,32,64]{0,2,1:T(8,128)(2,1)S(1)} %bitcast.95, ...), kind=kOutput, calls=%fused_computation.31 | convolution fusion | flops 287825920 | bytes 7798912 | tf_op jit(solution)/shard_map/hkts,kshp->kthp/dot_general | solution.py:87
  69.2 0.7 fusion.16
  69.9 17.1 %convolution_bitcast_fusion = f32[8192,256]{0,1:T(8,128)} fusion(bf16[256,2048]{0,1:T(8,128)(2,1)S(1)} %fusion.16, bf16[2048,8192]{1,0:T(8,128)(2,1)} %param.21), kind=kOutput, calls=%fused_computation.3 | convolution fusion | flops 8589934592 | bytes 42991616 | tf_op jit(solution)/shard_map/dot_general | solution.py:131
  87.0 0.0 reduce-scatter.2.cloned.1.call-update
  87.0 144.8 %reduce-scatter.2.cloned.1.call-done = f32[2048,256]{0,1:T(8,128)} async-done(((f32[8192,256]{0,1:T(8,128)}), f32[2048,256]{0,1:T(8,128)}) %reduce-scatter.2.cloned.1.call-update) | async-done | bytes 2097168 | tf_op jit(solution)/shard_map/reduce_scatter | solution.py:130
  231.8 2.7 %convert_bitcast_fusion = bf16[256,2048]{1,0:T(8,128)(2,1)} fusion(f32[2048,256]{0,1:T(8,128)} %reduce-scatter.2.cloned.1.call-done), kind=kLoop, calls=%fused_computation.37 | loop fusion | flops 524288 | bytes 3145728 | tf_op jit(solution)/shard_map/convert_element_type | solution.py:138
  (24 shorter events, 0.3 us)
Async XLA Ops:
  6.5 10.2 %copy-start.2 = (bf16[256,256]{1,0:T(8,128)(2,1)S(1)}, bf16[256,256]{1,0:T(8,128)(2,1)}, u32[]{:S(2)}) copy-start(bf16[256,256]{1,0:T(8,128)(2,1)} %param.13) | copy-start | bytes 393220
  6.5 53.6 %all-gather.4.cloned.1.call-start = ((), (), s32[]{:S(2)}) async-start(), calls=%async_computation.2 | async-start | bytes 5242880 | tf_op jit(solution)/shard_map/all_gather | solution.py:20
  8.1 8.6 %collective-permute-start = (bf16[3,2304]{1,0:T(4,128)(2,1)S(1)}, bf16[3,2304]{1,0:T(4,128)(2,1)S(1)}, u32[]{:S(2)}, u32[]{:S(2)}) collective-permute-start(bf16[3,2304]{1,0:T(4,128)(2,1)S(1)} %pad_maximum_fusion), channel_id=1, source_target_pairs={{0,1},{1,2},{2,3},{4,5},{5,6},{6,7},{8,9},{9,10},{10,11},{12,13},{... | collective-permute-start | bytes 41480 | tf_op jit(solution)/shard_map/ppermute | solution.py:15
  21.9 2.2 copy-start.5
  21.9 10.4 %copy-start = (bf16[256,2048]{1,0:T(8,128)(2,1)S(1)}, bf16[256,2048]{1,0:T(8,128)(2,1)}, u32[]{:S(2)}) copy-start(bf16[256,2048]{1,0:T(8,128)(2,1)} %param.14) | copy-start | bytes 3145732
  23.9 207.9 %reduce-scatter.2.cloned.1.call-start = ((), (), s32[]{:S(2)}) async-start(), calls=%async_computation.1 | async-start | bytes 10485760 | tf_op jit(solution)/shard_map/reduce_scatter | solution.py:130
  64.6 1.2 copy-start.1
  64.6 1.2 copy-start.4
  65.8 3.3 %copy-start.3 = (f32[2048]{0:T(1024)S(1)}, f32[2048]{0:T(1024)}, u32[]{:S(2)}) copy-start(f32[2048]{0:T(1024)} %param.20) | copy-start | bytes 24580
Sparse Core Ops, SparseCore 0:
  24.1 36.0 all-gather.3
  87.2 144.6 reduce-scatter.1
where the time goes:
time: 244 us; the launch traced here: 241 us
  waiting for transfers between devices  172 us (70%)
  matrix products  23.6 us (10%)
  other arithmetic  18 us (7%)
  between operations  14.4 us (6%)
  blocking collectives  6.56 us (3%)
  local copies, waits for them, and re-layouts  5.52 us (2%)
    reduce_scatter x1, waiting for transfers between devices, local(): lax.psum_scatter(lax.dot_general(out_weight, normed, (((0,), (1,)), ((),...  145 us
    all_gather x1, waiting for transfers between devices, entering(): pieces = jax.tree.map(lambda part: lax.all_gather(part, axis), value)  27.1 us
    dot_general x1, matrix products, local(): lax.dot_general(out_weight, normed, (((0,), (1,)), ((), ())), preferred_e...  17.1 us
    unnamed x1, blocking collectives  6.56 us
  transfers between devices with their start and end apart: 3, of which 2 were waited for; matrix products, arithmetic and copies ran while one was open for 4% of the time, Pallas kernels for 0%

commit v1 on v0

v1 whole, which is shorter than its diff:
```python
import functools

import jax
import jax.numpy as jnp
from jax import lax
from jax.experimental import pallas as pl
from jax.experimental.pallas import tpu as pltpu
from jax.sharding import PartitionSpec as P

MESH = pl.DeviceIdType.MESH
LOG2E = 1.4426950408889634
NEG = -1e30
LANES = 128
F32 = jnp.float32
BF16 = jnp.bfloat16


def silu(v):
    return 0.5 * v * (1.0 + jnp.tanh(0.5 * v))


def iota(shape, dim):
    return lax.broadcasted_iota(jnp.int32, shape, dim)


def dot(a, b, **kw):
    return jnp.dot(a, b, preferred_element_type=F32, **kw)


def kernel(
    sizes,
    x,
    maps,
    gate,
    step,
    decay,
    skip,
    taps,
    map_taps,
    gain,
    w_hbm,
    out,
    halo_x,
    halo_m,
    wide,
    conv,
    rows,
    decay_row,
    state,
    state_in,
    state_out,
    local_part,
    growth,
    normed,
    partial,
    from_left,
    from_right,
    wbuf,
    halo_sem,
    state_sem,
    w_sem,
    send_right,
    recv_right,
    send_left,
    recv_left,
):
    T, S, hd, np_, pw, nbuf = sizes
    tokens, C = x.shape
    half = tokens // 2
    Hp = step.shape[0]
    N = maps.shape[1] // 2
    lead = taps.shape[0] - 1
    tail = halo_x.shape[0]
    cols = np_ * pw
    total = T * np_
    m = lax.axis_index("tensor")
    me = lax.axis_index("seq")

    def piece_of(i):
        k, q = lax.div(i, np_), lax.rem(i, np_)
        return jnp.where(2 * m < T, T - 1 - k, k), q

    def w_copy(i, slot):
        c, q = piece_of(i)
        start = pl.multiple_of((c * np_ + q) * pw, pw)
        return pltpu.make_async_copy(w_hbm.at[:, pl.ds(start, pw)], wbuf.at[slot], w_sem.at[slot])

    for i in range(nbuf):
        w_copy(jnp.int32(i), i).start()

    barrier = pltpu.get_barrier_semaphore()
    for axis, mine, count in (("seq", me, S), ("tensor", m, T)):
        for other in (lax.rem(mine + 1, count), lax.rem(mine + count - 1, count)):
            pl.semaphore_signal(barrier, inc=1, device_id={axis: other}, device_id_type=MESH)
    pl.semaphore_wait(barrier, 4)

    after = lax.rem(me + 1, S)

    def halo_copies():
        return [
            pltpu.make_async_remote_copy(
                src_ref=src.at[pl.ds(tokens - tail, tail), :],
                dst_ref=dst,
                send_sem=halo_sem.at[0, k],
                recv_sem=halo_sem.at[1, k],
                device_id={"seq": after},
                device_id_type=MESH,
            )
            for k, (src, dst) in enumerate(((x, halo_x), (maps, halo_m)))
        ]

    @pl.when(me < S - 1)
    def _():
        for copy in halo_copies():
            copy.start()

    raw = step[...]
    size = jnp.maximum(raw, 0.0) + jnp.log1p(jnp.exp(-jnp.abs(raw)))
    log_decay = (-LOG2E * jnp.exp(decay[...])) * size
    upto = (iota((tokens, tokens), 0) <= iota((tokens, tokens), 1)).astype(F32)
    cum = dot(log_decay, upto, precision=lax.Precision.HIGHEST)
    shifted = cum - jnp.log(size) * LOG2E
    rows[...] = shifted
    last = cum[:, tokens - 1 : tokens]
    tail_weight = jnp.exp2(last - shifted)
    head_decay = jnp.exp2(last)
    hi = cum.astype(BF16).astype(F32)
    mid = (cum - hi).astype(BF16).astype(F32)
    low = cum - hi - mid
    spread = jnp.transpose(jnp.concatenate([hi, mid, low, tail_weight], axis=0)).astype(BF16)

    def in_head(count, width, start, group):
        offset = iota((count, width), 1) + start - (iota((count, width), 0) - group * Hp) * hd
        return (offset >= 0) & (offset < hd)

    def convolve(values, halo, kernel_taps, width):
        wide[0:8, :width] = halo
        wide[8:, :width] = values.astype(F32)
        k = kernel_taps.astype(F32)
        summed = k[0:1] * wide[8 - lead : 8 - lead + tokens, :width]
        for o in range(1, lead + 1):
            summed = summed + k[o : o + 1] * wide[8 - lead + o : 8 - lead + o + tokens, :width]
        return silu(summed)

    @pl.when(me > 0)
    def _():
        for copy in halo_copies():
            copy.wait_recv()

    @pl.when(me == 0)
    def _():
        halo_x[...] = jnp.zeros_like(halo_x)
        halo_m[...] = jnp.zeros_like(halo_m)
        state_in[...] = jnp.zeros_like(state_in)

    maps_out = convolve(maps[...], halo_m[...].astype(F32)[tail - 8 :], map_taps[...], 2 * N)
    b_t = jnp.transpose(maps_out[:, :N]).astype(BF16)
    c_mat = maps_out[:, N:].astype(BF16)
    scores = dot(c_mat, b_t)

    cw = min(C, 256)

    def states(i, carry):
        start = pl.multiple_of(i * cw, cw)
        ds = pl.ds(start, cw)
        value = convolve(x[:, ds], halo_x[:, ds].astype(F32)[tail - 8 :], taps[:, ds], cw).astype(
            BF16
        )
        conv[:, ds] = value
        spread_tail = dot(spread, in_head(4 * Hp, cw, start, 3).astype(BF16))
        weighted = (value.astype(F32) * spread_tail).astype(BF16)
        own = dot(b_t, weighted)
        state[:, ds] = own
        decay_row[:, ds] = jnp.sum(
            jnp.where(in_head(Hp, cw, start, 0), head_decay, 0.0), axis=0, keepdims=True
        )
        state_out[:, ds] = own.astype(BF16)
        return carry

    lax.fori_loop(0, C // cw, states, 0)

    def state_copy():
        return pltpu.make_async_remote_copy(
            src_ref=state_out,
            dst_ref=state_in,
            send_sem=state_sem.at[0],
            recv_sem=state_sem.at[1],
            device_id={"seq": after},
            device_id_type=MESH,
        )

    def relay():
        state_copy().wait_recv()

        @pl.when(me < S - 1)
        def _():
            state_out[...] = (decay_row[...] * state_in[...].astype(F32) + state[...]).astype(BF16)
            state_copy().start()

    @pl.when((me == 0) & (me < S - 1))
    def _():
        state_copy().start()

    @pl.when(me == 1)
    def _():
        relay()

    triangle = iota((half, half), 0) >= iota((half, half), 1)
    per = LANES // hd

    def inside(p, carry):
        start = pl.multiple_of(p * LANES, LANES)
        ds = pl.ds(start, LANES)
        member = (
            in_head(4 * Hp, LANES, start, 0)
            | in_head(4 * Hp, LANES, start, 1)
            | in_head(4 * Hp, LANES, start, 2)
        )
        column = dot(spread, member.astype(BF16))
        value = conv[:, ds].astype(F32)
        lane = iota((tokens, LANES), 1)
        top = jnp.zeros((half, LANES), F32)
        bottom = jnp.zeros((half, LANES), F32)
        for j in range(per):
            row = rows[pl.ds(p * per + j, 1), :]
            mine = column[:, j * hd : j * hd + 1]
            own = jnp.where((lane >= j * hd) & (lane < (j + 1) * hd), value, 0.0).astype(BF16)
            first = jnp.where(triangle, mine[:half] - row[:, :half], NEG)
            w_first = (scores[:half, :half] * jnp.exp2(first)).astype(BF16)
            top = top + dot(w_first, own[:half])
            w_left = (scores[half:, :half] * jnp.exp2(mine[half:] - row[:, :half])).astype(BF16)
            second = jnp.where(triangle, mine[half:] - row[:, half:], NEG)
            w_right = (scores[half:, half:] * jnp.exp2(second)).astype(BF16)
            bottom = bottom + dot(w_left, own[:half]) + dot(w_right, own[half:])
        skip_row = jnp.sum(
            jnp.where(in_head(Hp, LANES, start, 0), skip[...], 0.0), axis=0, keepdims=True
        )
        gated = silu(gate[:, ds].astype(F32))
        joined = jnp.concatenate([top, bottom], axis=0)
        local_part[:, ds] = (joined + skip_row * value) * gated
        growth[:, ds] = jnp.exp2(column) * gated
        return carry

    lax.fori_loop(0, C // LANES, inside, 0)

    @pl.when(me > 1)
    def _():
        relay()

    same_head = None
    for j in range(per):
        block = lambda d: (iota((LANES, LANES), d) >= j * hd) & (
            iota((LANES, LANES), d) < (j + 1) * hd
        )
        both = block(0) & block(1)
        same_head = both if same_head is None else same_head | both
    same_head = same_head.astype(BF16)

    def finish(p, carry):
        ds = pl.ds(pl.multiple_of(p * LANES, LANES), LANES)
        y = local_part[:, ds] + dot(c_mat, state_in[:, ds]) * growth[:, ds]
        mean = dot((y * y).astype(BF16), same_head) * (1.0 / hd)
        normed[:, ds] = (y * lax.rsqrt(mean + 1e-05) * gain[:, ds]).astype(BF16)
        return carry

    lax.fori_loop(0, C // LANES, finish, 0)

    right, left = lax.rem(m + 1, T), lax.rem(m + T - 1, T)

    def send(rightward, slot, index):
        buffer, ssem, rsem, to = (
            (from_left, send_right, recv_right, right)
            if rightward
            else (from_right, send_left, recv_left, left)
        )
        return pltpu.make_async_remote_copy(
            src_ref=partial.at[index],
            dst_ref=buffer.at[slot],
            send_sem=ssem.at[slot],
            recv_sem=rsem.at[slot],
            device_id={"tensor": to},
            device_id_type=MESH,
        )

    def project(i, carry):
        slot = lax.rem(i, nbuf)
        c, q = piece_of(i)
        index = c * np_ + q
        w_copy(i, slot).wait()
        result = dot(normed[...], wbuf[slot]).astype(BF16)

        @pl.when(c == m)
        def _():
            out[:, pl.ds(pl.multiple_of(q * pw, pw), pw)] = result

        @pl.when(c != m)
        def _():
            partial[index] = result

        @pl.when((m == 0) & (c != m))
        def _():
            send(True, i, index).start()

        @pl.when((m == T - 1) & (c != m))
        def _():
            send(False, i, index).start()

        @pl.when(i + nbuf < total)
        def _():
            w_copy(i + nbuf, slot).start()

        return carry

    lax.fori_loop(0, total, project, 0)

    def arrive(rightward, slot, buffer):
        k, q = lax.div(slot, np_), lax.rem(slot, np_)
        c = T - 1 - k if rightward else k
        index = c * np_ + q
        send(rightward, slot, index).wait_recv()

        @pl.when(c == m)
        def _():
            ds = pl.ds(pl.multiple_of(q * pw, pw), pw)
            out[:, ds] = (out[:, ds].astype(F32) + buffer[slot].astype(F32)).astype(BF16)

        @pl.when(c != m)
        def _():
            partial[index] = (partial[index].astype(F32) + buffer[slot].astype(F32)).astype(BF16)
            send(rightward, slot, index).start()

    def exchange(t, carry):
        to_right = t - m
        to_left = t - (T - 1 - m)

        @pl.when((m > 0) & (to_right >= 0) & (to_right < (T - m) * np_))
        def _():
            arrive(True, to_right, from_left)

        @pl.when((m < T - 1) & (to_left >= 0) & (to_left < (m + 1) * np_))
        def _():
            arrive(False, to_left, from_right)

        return carry

    lax.fori_loop(1, total + 1, exchange, 0)

    def drain(slot, carry):
        @pl.when(slot < (T - 1 - m) * np_)
        def _():
            send(True, slot, 0).wait_send()

        @pl.when(slot < m * np_)
        def _():
            send(False, slot, 0).wait_send()

        return carry

    lax.fori_loop(0, total, drain, 0)

    @pl.when(me < S - 1)
    def _():
        for copy in halo_copies():
            copy.wait_send()
        state_copy().wait_send()


def local(
    sizes,
    mixer_input,
    state_maps,
    gate_input,
    step_raw,
    decay_log,
    skip_gain,
    conv_input,
    conv_maps,
    norm_gain,
    out_weight,
):
    T, S = sizes
    tokens, C = mixer_input.shape
    H = decay_log.shape[0]
    hd = C // H
    two_n = state_maps.shape[1]
    n = two_n // 2
    cols = out_weight.shape[1] // T
    pw = min(cols, 512)
    np_ = cols // pw
    total = T * np_
    nbuf = min(4, total)
    pad = -H % 8
    column = lambda a: jnp.pad(a, (0, pad)).reshape(H + pad, 1)
    Hp = H + pad
    vmem = pl.BlockSpec(memory_space=pltpu.VMEM)
    dma = pltpu.SemaphoreType.DMA
    return pl.pallas_call(
        functools.partial(kernel, (T, S, hd, np_, pw, nbuf)),
        out_shape=jax.ShapeDtypeStruct((tokens, cols), BF16),
        in_specs=[vmem] * 9 + [pl.BlockSpec(memory_space=pl.ANY)],
        out_specs=vmem,
        scratch_shapes=[
            pltpu.VMEM((16, C), BF16),
            pltpu.VMEM((16, two_n), BF16),
            pltpu.VMEM((tokens + 8, max(two_n, min(C, 256))), F32),
            pltpu.VMEM((tokens, C), BF16),
            pltpu.VMEM((Hp, tokens), F32),
            pltpu.VMEM((1, C), F32),
            pltpu.VMEM((n, C), F32),
            pltpu.VMEM((n, C), BF16),
            pltpu.VMEM((n, C), BF16),
            pltpu.VMEM((tokens, C), F32),
            pltpu.VMEM((tokens, C), F32),
            pltpu.VMEM((tokens, C), BF16),
            pltpu.VMEM((total, tokens, pw), BF16),
            pltpu.VMEM((total, tokens, pw), BF16),
            pltpu.VMEM((total, tokens, pw), BF16),
            pltpu.VMEM((nbuf, C, pw), BF16),
            dma((2, 2)),
            dma((2,)),
            dma((nbuf,)),
            dma((total,)),
            dma((total,)),
            dma((total,)),
            dma((total,)),
        ],
        compiler_params=pltpu.CompilerParams(
            collective_id=0, has_side_effects=True, vmem_limit_bytes=60 * 1024 * 1024
        ),
    )(
        mixer_input,
        state_maps,
        gate_input,
        jnp.pad(step_raw, ((0, pad), (0, 0))),
        column(decay_log),
        column(skip_gain),
        conv_input,
        conv_maps,
        norm_gain.reshape(1, C),
        out_weight,
    )


def solution(mesh):
    placed = (
        P(("group", "seq"), "tensor"),
        P(("group", "seq"), None),
        P(("group", "seq"), "tensor"),
        P("tensor", ("group", "seq")),
        P("tensor"),
        P("tensor"),
        P(None, "tensor"),
        P(),
        P("tensor"),
        P("tensor", None),
    )
    return jax.shard_map(
        functools.partial(local, (mesh.shape["tensor"], mesh.shape["seq"])),
        mesh=mesh,
        in_specs=placed,
        out_specs=P(("group", "seq"), "tensor"),
        check_vma=False,
    )
```

time: 244 us -> 101 us (0.41); the launches traced: 241 us -> 101 us
  waiting for transfers between devices: 172 us -> 0 us
  Pallas kernels: 0 us -> 96.3 us
  matrix products: 23.6 us -> 0 us
  other arithmetic: 18 us -> 0 us
  between operations: 14.4 us -> 0.01 us
  blocking collectives: 6.56 us -> 0 us
    reduce_scatter x1 -> x0, waiting for transfers between devices: 145 us -> none  [local(): lax.psum_scatter(lax.dot_general(out_weight, normed, (((0,), (1,)), ((),...]
    pallas_call x0 -> x1, Pallas kernels: none -> 96.3 us  [local(): pl.pallas_call(functools.partial(kernel, (T, S, hd, np_, pw, nbuf)), out_...]
    all_gather x1 -> x0, waiting for transfers between devices: 27.1 us -> none  [entering(): pieces = jax.tree.map(lambda part: lax.all_gather(part, axis), value)]
    dot_general x5 -> x0, matrix products: 23.6 us -> none  [the longest x1 17.1 us: local(): lax.dot_general(out_weight, normed, (((0,), (1,)), ((), ())), preferred_e...]
    mul x5 -> x0, other arithmetic: 7.03 us -> none  [the longest x2 4.69 us: local(): value_blocks.astype(jnp.float32)]
    unnamed x1 -> x0, blocking collectives: 6.56 us -> none
    select_n x4 -> x0, other arithmetic: 5.22 us -> none  [the longest x3 4.39 us: step(): jnp.where(position < mine, new, old)]
    convert_element_type x5 -> x0, other arithmetic: 4.36 us -> none  [the longest x1 2.71 us: local(): return owned_rows.T.astype(jnp.bfloat16)]
  transfers between devices with their start and end apart: 3 -> 0, of which waited for: 2 -> 0; matrix products, arithmetic and copies ran while one was open for 4% -> 0% of each run, Pallas kernels for 0% -> 0%
where the time goes in v1:
time: 101 us
  Pallas kernels  96.3 us (95%)
  local copies, waits for them, and re-layouts  4.98 us (5%)
    pallas_call x1, Pallas kernels, local(): pl.pallas_call(functools.partial(kernel, (T, S, hd, np_, pw, nbuf)), out_...  96.3 us
    reshape x2, local copies, waits for them, and re-layouts, local(): column = lambda a: jnp.pad(a, (0, pad)).reshape(H + pad, 1)  2.67 us
    unnamed x1, local copies, waits for them, and re-layouts  2.3 us

profile of v1, /device:TPU:11, one launch (start us, length us, event | category | flops | bytes accessed | tf_op | source)
XLA Modules:
  0.0 101.3 jit_solution(9097178936212776185)
XLA Ops:
  0.0 1.3 %copy.11.decay = f32[32,1]{1,0:T(8,128)} copy(f32[32,1]{0,1:T(1,128)} %bitcast.4) | data formatting | bytes 256 | tf_op jit(solution)/shard_map/reshape | solution.py:393
  1.3 1.3 %copy.12.skip = f32[32,1]{1,0:T(8,128)} copy(f32[32,1]{0,1:T(1,128)} %bitcast.5) | data formatting | bytes 256 | tf_op jit(solution)/shard_map/reshape | solution.py:393
  2.7 96.3 %shard_map.100 = bf16[256,2048]{1,0:T(8,128)(2,1)} custom-call(bf16[256,2048]{1,0:T(8,128)(2,1)} %x.1, bf16[256,256]{1,0:T(8,128)(2,1)} %maps.1, bf16[256,2048]{1,0:T(8,128)(2,1)} %gate.1, f32[32,256]{1,0:T(8,128)} %step.1, f32[32,1]{1,0:T(8,128)} %copy.11.decay, f32[32,1]{1,0:T(8,128)} %copy.12.skip, bf16[4,2048]{1,0:T(4,128)(2,1)} %taps.1, ...), custom_call_target="tpu_custom_call" | custom-call | tf_op jit(solution)/shard_map/pallas_call | solution.py:397
  99.0 2.3 %copy.14 = bf16[256,2048]{1,0:T(8,128)(2,1)} copy(bf16[256,2048]{1,0:T(8,128)(2,1)} %shard_map.100) | data formatting | bytes 2097152

commit v2 on v1

--- a/solution.py
+++ b/solution.py
@@ -29,41 +29,36 @@
 
 def kernel(
     sizes,
-    x,
-    maps,
-    gate,
-    step,
-    decay,
-    skip,
-    taps,
-    map_taps,
-    gain,
-    w_hbm,
-    out,
-    halo_x,
-    halo_m,
-    wide,
-    conv,
-    rows,
-    decay_row,
-    state,
-    state_in,
-    state_out,
-    local_part,
-    growth,
-    normed,
-    partial,
-    from_left,
-    from_right,
-    wbuf,
-    halo_sem,
-    state_sem,
-    w_sem,
-    send_right,
-    recv_right,
-    send_left,
-    recv_left,
+    *refs,
 ):
+    sources, w_hbm, out, held = refs[:9], refs[9], refs[10], refs[11:20]
+    x, maps, gate, step, decay, skip, taps, map_taps, gain = held
+    (
+        halo_x,
+        halo_m,
+        wide,
+        conv,
+        rows,
+        decay_row,
+        state,
+        state_in,
+        state_out,
+        local_part,
+        growth,
+        normed,
+        partial,
+        from_left,
+        from_right,
+        wbuf,
+        halo_sem,
+        state_sem,
+        w_sem,
+        send_right,
+        recv_right,
+        send_left,
+        recv_left,
+        in_sem,
+    ) = refs[20:]
     T, S, hd, np_, pw, nbuf = sizes
     tokens, C = x.shape
     half = tokens // 2
@@ -85,6 +80,11 @@
         start = pl.multiple_of((c * np_ + q) * pw, pw)
         return pltpu.make_async_copy(w_hbm.at[:, pl.ds(start, pw)], wbuf.at[slot], w_sem.at[slot])
 
+    loads = [
+        pltpu.make_async_copy(src, dst, in_sem.at[k]) for k, (src, dst) in enumerate(zip(sources, held))
+    ]
+    for load in loads:
+        load.start()
     for i in range(nbuf):
         w_copy(jnp.int32(i), i).start()
 
@@ -95,6 +95,8 @@
     pl.semaphore_wait(barrier, 4)
 
     after = lax.rem(me + 1, S)
+    for load in loads:
+        load.wait()
 
     def halo_copies():
         return [
@@ -114,13 +116,22 @@
         for copy in halo_copies():
             copy.start()
 
+    def upright(row):
+        heads = row.shape[1]
+        return jnp.sum(
+            jnp.where(iota((Hp, heads), 0) == iota((Hp, heads), 1), row[...], 0.0),
+            axis=1,
+            keepdims=True,
+        )
+
     raw = step[...]
     size = jnp.maximum(raw, 0.0) + jnp.log1p(jnp.exp(-jnp.abs(raw)))
-    log_decay = (-LOG2E * jnp.exp(decay[...])) * size
+    log_decay = (-LOG2E * jnp.exp(upright(decay))) * size
     upto = (iota((tokens, tokens), 0) <= iota((tokens, tokens), 1)).astype(F32)
     cum = dot(log_decay, upto, precision=lax.Precision.HIGHEST)
     shifted = cum - jnp.log(size) * LOG2E
     rows[...] = shifted
+    skips = upright(skip)
     last = cum[:, tokens - 1 : tokens]
     tail_weight = jnp.exp2(last - shifted)
     head_decay = jnp.exp2(last)
@@ -158,7 +169,27 @@
     c_mat = maps_out[:, N:].astype(BF16)
     scores = dot(c_mat, b_t)
 
-    cw = min(C, 256)
+    cw = state.shape[2]
+    chunks = C // cw
+
+    def state_copy(i):
+        return pltpu.make_async_remote_copy(
+            src_ref=state_out.at[i],
+            dst_ref=state_in.at[i],
+            send_sem=state_sem.at[0, i],
+            recv_sem=state_sem.at[1, i],
+            device_id={"seq": after},
+            device_id_type=MESH,
+        )
+
+    def relay(i):
+        state_copy(i).wait_recv()
+
+        @pl.when(me < S - 1)
+        def _():
+            decayed = decay_row[:, pl.ds(pl.multiple_of(i * cw, cw), cw)]
+            state_out[i] = (decayed * state_in[i].astype(F32) + state[i]).astype(BF16)
+            state_copy(i).start()
 
     def states(i, carry):
         start = pl.multiple_of(i * cw, cw)
@@ -170,40 +201,30 @@
         spread_tail = dot(spread, in_head(4 * Hp, cw, start, 3).astype(BF16))
         weighted = (value.astype(F32) * spread_tail).astype(BF16)
         own = dot(b_t, weighted)
-        state[:, ds] = own
         decay_row[:, ds] = jnp.sum(
             jnp.where(in_head(Hp, cw, start, 0), head_decay, 0.0), axis=0, keepdims=True
         )
-        state_out[:, ds] = own.astype(BF16)
-        return carry
-
-    lax.fori_loop(0, C // cw, states, 0)
-
-    def state_copy():
-        return pltpu.make_async_remote_copy(
-            src_ref=state_out,
-            dst_ref=state_in,
-            send_sem=state_sem.at[0],
-            recv_sem=state_sem.at[1],
-            device_id={"seq": after},
-            device_id_type=MESH,
-        )
-
-    def relay():
-        state_copy().wait_recv()
-
-        @pl.when(me < S - 1)
-        def _():
-            state_out[...] = (decay_row[...] * state_in[...].astype(F32) + state[...]).astype(BF16)
-            state_copy().start()
-
-    @pl.when((me == 0) & (me < S - 1))
-    def _():
-        state_copy().start()
+
+        @pl.when(me > 0)
+        def _():
+            state[i] = own
+
+        @pl.when((me == 0) & (me < S - 1))
+        def _():
+            state_out[i] = own.astype(BF16)
+            state_copy(i).start()
+
+        @pl.when((me == 1) & (i > 0))
+        def _():
+            relay(jnp.maximum(i - 1, 0))
+
+        return carry
+
+    lax.fori_loop(0, chunks, states, 0)
 
     @pl.when(me == 1)
     def _():
-        relay()
+        relay(chunks - 1)
 
     triangle = iota((half, half), 0) >= iota((half, half), 1)
     per = LANES // hd
@@ -233,7 +254,7 @@
             w_right = (scores[half:, half:] * jnp.exp2(second)).astype(BF16)
             bottom = bottom + dot(w_left, own[:half]) + dot(w_right, own[half:])
         skip_row = jnp.sum(
-            jnp.where(in_head(Hp, LANES, start, 0), skip[...], 0.0), axis=0, keepdims=True
+            jnp.where(in_head(Hp, LANES, start, 0), skips, 0.0), axis=0, keepdims=True
         )
         gated = silu(gate[:, ds].astype(F32))
         joined = jnp.concatenate([top, bottom], axis=0)
@@ -243,10 +264,6 @@
 
     lax.fori_loop(0, C // LANES, inside, 0)
 
-    @pl.when(me > 1)
-    def _():
-        relay()
-
     same_head = None
     for j in range(per):
         block = lambda d: (iota((LANES, LANES), d) >= j * hd) & (
@@ -256,14 +273,20 @@
         same_head = both if same_head is None else same_head | both
     same_head = same_head.astype(BF16)
 
-    def finish(p, carry):
-        ds = pl.ds(pl.multiple_of(p * LANES, LANES), LANES)
-        y = local_part[:, ds] + dot(c_mat, state_in[:, ds]) * growth[:, ds]
-        mean = dot((y * y).astype(BF16), same_head) * (1.0 / hd)
-        normed[:, ds] = (y * lax.rsqrt(mean + 1e-05) * gain[:, ds]).astype(BF16)
-        return carry
-
-    lax.fori_loop(0, C // LANES, finish, 0)
+    def finish(i, carry):
+        @pl.when(me > 1)
+        def _():
+            relay(i)
+
+        for k in range(0, cw, LANES):
+            ds = pl.ds(pl.multiple_of(i * cw + k, LANES), LANES)
+            incoming = dot(c_mat, state_in[i, :, k : k + LANES])
+            y = local_part[:, ds] + incoming * growth[:, ds]
+            mean = dot((y * y).astype(BF16), same_head) * (1.0 / hd)
+            normed[:, ds] = (y * lax.rsqrt(mean + 1e-05) * gain[:, ds]).astype(BF16)
+        return carry
+
+    lax.fori_loop(0, chunks, finish, 0)
 
     right, left = lax.rem(m + 1, T), lax.rem(m + T - 1, T)
 
@@ -362,7 +385,8 @@
     def _():
         for copy in halo_copies():
             copy.wait_send()
-        state_copy().wait_send()
+        for i in range(chunks):
+            state_copy(i).wait_send()
 
 
 def local(
@@ -390,25 +414,38 @@
     total = T * np_
     nbuf = min(4, total)
     pad = -H % 8
-    column = lambda a: jnp.pad(a, (0, pad)).reshape(H + pad, 1)
+    cw = min(C, 256)
     Hp = H + pad
+    operands = (
+        mixer_input,
+        state_maps,
+        gate_input,
+        jnp.pad(step_raw, ((0, pad), (0, 0))),
+        decay_log.reshape(1, H),
+        skip_gain.reshape(1, H),
+        conv_input,
+        conv_maps,
+        norm_gain.reshape(1, C),
+        out_weight,
+    )
     vmem = pl.BlockSpec(memory_space=pltpu.VMEM)
     dma = pltpu.SemaphoreType.DMA
     return pl.pallas_call(
         functools.partial(kernel, (T, S, hd, np_, pw, nbuf)),
-        out_shape=jax.ShapeDtypeStruct((tokens, cols), BF16),
-        in_specs=[vmem] * 9 + [pl.BlockSpec(memory_space=pl.ANY)],
+        out_shape=pltpu.VMEM((tokens, cols), BF16),
+        in_specs=[pl.BlockSpec(memory_space=pltpu.HBM)] * 10,
         out_specs=vmem,
-        scratch_shapes=[
+        scratch_shapes=[pltpu.VMEM(a.shape, a.dtype) for a in operands[:9]]
+        + [
             pltpu.VMEM((16, C), BF16),
             pltpu.VMEM((16, two_n), BF16),
-            pltpu.VMEM((tokens + 8, max(two_n, min(C, 256))), F32),
+            pltpu.VMEM((tokens + 8, max(two_n, cw)), F32),
             pltpu.VMEM((tokens, C), BF16),
             pltpu.VMEM((Hp, tokens), F32),
             pltpu.VMEM((1, C), F32),
-            pltpu.VMEM((n, C), F32),
-            pltpu.VMEM((n, C), BF16),
-            pltpu.VMEM((n, C), BF16),
+            pltpu.VMEM((C // cw, n, cw), F32),
+            pltpu.VMEM((C // cw, n, cw), BF16),
+            pltpu.VMEM((C // cw, n, cw), BF16),
             pltpu.VMEM((tokens, C), F32),
             pltpu.VMEM((tokens, C), F32),
             pltpu.VMEM((tokens, C), BF16),
@@ -417,28 +454,18 @@
             pltpu.VMEM((total, tokens, pw), BF16),
             pltpu.VMEM((nbuf, C, pw), BF16),
             dma((2, 2)),
-            dma((2,)),
+            dma((2, C // cw)),
             dma((nbuf,)),
             dma((total,)),
             dma((total,)),
             dma((total,)),
             dma((total,)),
+            dma((9,)),
         ],
         compiler_params=pltpu.CompilerParams(
-            collective_id=0, has_side_effects=True, vmem_limit_bytes=60 * 1024 * 1024
+            collective_id=0, has_side_effects=True, vmem_limit_bytes=65900000
         ),
-    )(
-        mixer_input,
-        state_maps,
-        gate_input,
-        jnp.pad(step_raw, ((0, pad), (0, 0))),
-        column(decay_log),
-        column(skip_gain),
-        conv_input,
-        conv_maps,
-        norm_gain.reshape(1, C),
-        out_weight,
-    )
+    )(*operands)
 
 
 def solution(mesh):

time: 101 us -> 93.6 us (0.927); the launches traced: 101 us -> 92.3 us
  Pallas kernels: 96.3 us -> 91.4 us
  local copies, waits for them, and re-layouts: 4.98 us -> 0.97 us
    pallas_call x1, Pallas kernels: 96.3 us -> 91.4 us  [local(): pl.pallas_call(functools.partial(kernel, (T, S, hd, np_, pw, nbuf)), out_...]
    reshape x2 -> x0, local copies, waits for them, and re-layouts: 2.67 us -> none  [local(): column = lambda a: jnp.pad(a, (0, pad)).reshape(H + pad, 1)]
    unnamed x1, local copies, waits for them, and re-layouts: 2.3 us -> 0.97 us
where the time goes in v2:
time: 93.6 us; the launch traced here: 92.3 us
  Pallas kernels  91.4 us (98%)
  local copies, waits for them, and re-layouts  0.97 us (1%)
    pallas_call x1, Pallas kernels, local(): pl.pallas_call(functools.partial(kernel, (T, S, hd, np_, pw, nbuf)), out_...  91.4 us

profile of v2, /device:TPU:11, one launch (start us, length us, event | category | flops | bytes accessed | tf_op | source)
XLA Modules:
  0.0 92.3 jit_solution(6231558713373947763)
XLA Ops:
  0.0 91.4 %shard_map.100 = bf16[256,2048]{1,0:T(8,128)(2,1)S(1)} custom-call(bf16[256,2048]{1,0:T(8,128)(2,1)} %refs_0_.1, bf16[256,256]{1,0:T(8,128)(2,1)} %refs_1_.1, bf16[256,2048]{1,0:T(8,128)(2,1)} %refs_2_.1, f32[32,256]{1,0:T(8,128)} %refs_3_.1, f32[1,32]{1,0:T(1,128)} %bitcast.4, f32[1,32]{1,0:T(1,128)} %bitcast.5, bf16[4,2048]{1,0:T(4,128)(2,1)} %refs_6_.1, ...), custom_call_target="tpu_custom_call" | custom-call | tf_op jit(solution)/shard_map/pallas_call | solution.py:433
  91.4 1.0 %copy.12 = bf16[256,2048]{1,0:T(8,128)(2,1)} copy(bf16[256,2048]{1,0:T(8,128)(2,1)S(1)} %shard_map.100) | data formatting | bytes 2097152
